TPU v7x, 32 devices: a whole 2x2x4 slice. The times are simulated.
32 devices in a mesh: groups: 2 (over y), range: 8 (over z, x), sub: 2 (over core).
Axes of the slice: x: 2, y: 2, z: 4, core: 2. Of those that a mesh axis runs over, the one named last changes fastest.
Arguments:
- samples: float32 [2, 1024, 32, 128], P(None, ('groups', 'range', 'sub')), parts along dimension 1, may hold values from -6 to 6
- beam_weights: float32 [32, 8, 2, 64, 128], P(('groups', 'range'), None, None, None, 'sub'), parts along dimension 0, may hold values from -0.25 to 0.25
- subarrays: int32 [32, 8, 64], P(('groups', 'range', 'sub')), parts along dimension 0, may hold values from 0 to 511, as said below
- training: int32 [64], P(('groups', 'range', 'sub')), parts along dimension 0, may hold values 0 or 1
Outputs:
- covariance: float32 [32, 8, 64, 128], P(('groups', 'range', 'sub')), parts along dimension 0
- filtered: float32 [2, 128, 64, 128], P(None, None, ('groups', 'range', 'sub')), parts along dimension 2
- energy: float32 [256], P('groups'), parts along dimension 0
There are 2 independent parts, one for each index of `groups`. A program takes and returns all parts, laid end to end along the dimension named above; each array names one. Nothing has to cross between parts.
Inputs may be any that keep to these rules, and one draw needn't show every extreme that they name: `subarrays`: in each gate block the 512 indices are all 512 channels, each once.
All inputs are finite; a program needn't handle non-finite values. No bound on the sum of `training` on one device may be relied on, other than what follows from the above.
Results may differ from a plain program's by a relative error of at most 0.0003.
Values sent between devices are 32-bit elements; how exact they have to be, the bound alone decides.
A program may use at most 64 MiB of HBM per device.

v0:
```python
import jax
import jax.numpy as jnp
from jax import lax
from jax.sharding import PartitionSpec as P

GB = 2
loading = 0.05


def block_terms(snaps, chosen, weights, masked, factor):
    highest = lax.Precision.HIGHEST
    picked = jnp.take(snaps, chosen, axis=1)
    real_part = picked[0]
    imag_part = picked[1]
    real_masked = real_part * masked
    imag_masked = imag_part * masked
    cov_real = (
        jnp.einsum("snx,smx->snm", real_masked, real_part, precision=highest)
        + jnp.einsum("snx,smx->snm", imag_masked, imag_part, precision=highest)
    ) * factor
    cov_imag = (
        jnp.einsum("snx,smx->snm", imag_masked, real_part, precision=highest)
        - jnp.einsum("snx,smx->snm", real_masked, imag_part, precision=highest)
    ) * factor
    w_real = weights[:, 0]
    w_imag = weights[:, 1]
    out_real = jnp.einsum("snk,snx->kx", w_real, real_part, precision=highest) + jnp.einsum(
        "snk,snx->kx", w_imag, imag_part, precision=highest
    )
    out_imag = jnp.einsum("snk,snx->kx", w_real, imag_part, precision=highest) - jnp.einsum(
        "snk,snx->kx", w_imag, real_part, precision=highest
    )
    prod_real = jnp.einsum("snm,smk->snk", cov_real, w_real, precision=highest) - jnp.einsum(
        "snm,smk->snk", cov_imag, w_imag, precision=highest
    )
    prod_imag = jnp.einsum("snm,smk->snk", cov_real, w_imag, precision=highest) + jnp.einsum(
        "snm,smk->snk", cov_imag, w_real, precision=highest
    )
    quadratic = jnp.sum(w_real * prod_real + w_imag * prod_imag, axis=(0, 1))
    inverse = 1.0 / jnp.sqrt(quadratic + loading)
    filtered = jnp.stack([out_real * inverse[:, None], out_imag * inverse[:, None]])
    energy = jnp.sum(out_real * out_real + out_imag * out_imag, axis=1)
    covariance = jnp.concatenate([cov_real, cov_imag], axis=-1)
    return (covariance, filtered, energy)


def body(samples, beam_weights, subarrays, training):
    range_count = lax.axis_size("range")
    core_count = lax.axis_size("sub")
    parts_iq, chan_dev, all_gates, pulses = samples.shape
    gate_dev = all_gates // (range_count * core_count)
    channels = chan_dev * range_count * core_count
    blocks_dev = gate_dev // GB
    spread = samples.reshape(parts_iq, 1, 1, chan_dev, range_count, core_count, gate_dev, pulses)
    turned = lax.all_to_all(
        lax.all_to_all(spread, "range", split_axis=4, concat_axis=1, tiled=True),
        "sub",
        split_axis=5,
        concat_axis=2,
        tiled=True,
    )
    local_data = turned.reshape(parts_iq, channels, blocks_dev, GB * pulses).transpose(2, 0, 1, 3)
    mine = lax.all_to_all(beam_weights, "sub", split_axis=0, concat_axis=4, tiled=True)
    gates_on = training.astype(jnp.float32).reshape(blocks_dev, GB)
    masked = jnp.repeat(gates_on, pulses, axis=1)
    factor = 1.0 / (GB * pulses)
    covs, filts, energies = jax.vmap(block_terms, in_axes=(0, 0, 0, 0, None))(
        local_data, subarrays, mine, masked, factor
    )
    beams = filts.shape[2]
    filtered = filts.reshape(blocks_dev, parts_iq, beams, GB, pulses).transpose(1, 2, 0, 3, 4)
    filtered = filtered.reshape(parts_iq, beams, gate_dev, pulses)
    total = lax.psum(jnp.sum(energies, axis=0), ("range", "sub"))
    energy = total / (all_gates * pulses)
    return (covs, filtered, energy)


def solution(mesh):
    placed = (
        P(None, ("groups", "range", "sub"), None, None),
        P(("groups", "range"), None, None, None, "sub"),
        P(("groups", "range", "sub"), None, None),
        P(("groups", "range", "sub")),
    )
    return jax.shard_map(
        body,
        mesh=mesh,
        in_specs=placed,
        out_specs=(
            P(("groups", "range", "sub"), None, None, None),
            P(None, None, ("groups", "range", "sub"), None),
            P("groups"),
        ),
        check_vma=False,
    )
```

profile of v0, /device:TPU:0, one launch (start us, length us, event | category | flops | bytes accessed | tf_op | source)
XLA Modules:
  0.0 92.5 jit_solution(9004139148378862796)
XLA Ops:
  0.6 0.0 copy-start
  0.6 2.5 %reshape.157 = f32[2,1,65536]{2,1,0:T(1,128)} reshape(f32[2,8,2,64,64]{4,3,2,1,0:T(8,128)} %param.5) | data formatting | bytes 1048576
  3.2 3.5 %all-to-all-start.2 = ((f32[2,1,65536]{2,1,0:T(1,128)}), f32[2,1,65536]{2,1,0:T(1,128)S(1)}, u32[]{:S(2)}, u32[]{:S(2)}) async-start(f32[2,1,65536]{2,1,0:T(1,128)} %reshape.157), calls=%async_computation.2 | async-start | bytes 1048576 | tf_op jit(solution)/shard_map/all_to_all | solution.py:63
  6.6 0.0 copy-done
  6.7 1.6 %copy.24 = f32[2,1,1,32,8,2,2,128]{7,6,3,5,0,2,1,4:T(2,128)} copy(f32[2,1,1,32,8,2,2,128]{7,6,5,4,3,0,2,1:T(2,128)S(1)} %bitcast.103) | data formatting | bytes 2097152 | tf_op jit(solution)/shard_map/reshape | solution.py:54
  8.2 0.0 copy-start.2
  8.2 0.2 all-to-all-done.2
  8.4 0.0 copy-start.1
  8.4 7.4 %all-to-all-start = ((f32[2,1,1,32,8,2,2,128]{7,6,3,5,0,2,1,4:T(2,128)}), f32[2,1,1,32,8,2,2,128]{7,6,3,5,0,2,1,4:T(2,128)S(1)}, u32[]{:S(2)}, u32[]{:S(2)}) async-start(f32[2,1,1,32,8,2,2,128]{7,6,3,5,0,2,1,4:T(2,128)} %copy.24), calls=%async_computation | async-start | bytes 2097152 | tf_op jit(solution)/shard_map/all_to_all | solution.py:56
  15.8 0.0 copy-done.2
  15.8 0.0 copy-done.1
  15.9 0.1 reshape.147
  15.9 0.5 broadcast.75
  16.4 2.3 %reduce.5 = f32[2,65536]{1,0:T(2,128)S(1)} reduce(f32[2,1,65536]{2,1,0:T(1,128)S(1)} %all-to-all-done.2, f32[]{:T(128)} %broadcast.75), dimensions={1}, to_apply=%all_to_all.44.reduce_sub_computation | reduce | bytes 1048580 | tf_op jit(solution)/shard_map/all_to_all | solution.py:63
  18.8 0.6 reshape.158
  19.4 1.9 %copy.29 = f32[1,8,2,64,2,64]{5,4,3,1,2,0:T(2,128)} copy(f32[1,8,2,64,2,64]{5,3,2,1,4,0:T(8,128)S(1)} %bitcast.98) | data formatting | bytes 1048576 | tf_op jit(solution)/shard_map/all_to_all | solution.py:63
  21.2 1.8 %all_to_all.47 = f32[1,8,2,64,128]{4,3,1,2,0:T(8,128)S(1)} reshape(f32[1,8,2,64,2,64]{5,4,3,1,2,0:T(2,128)} %copy.29) | data formatting | bytes 1048576 | tf_op jit(solution)/shard_map/all_to_all | solution.py:63
  23.1 0.1 broadcast_bitcast_fusion
  23.1 18.9 %all-to-all-done = f32[2,1,1,32,8,2,2,128]{7,6,3,5,0,2,1,4:T(2,128)S(1)} async-done(((f32[2,1,1,32,8,2,2,128]{7,6,3,5,0,2,1,4:T(2,128)}), f32[2,1,1,32,8,2,2,128]{7,6,3,5,0,2,1,4:T(2,128)S(1)}, u32[]{:S(2)}, u32[]{:S(2)}) %all-to-all-start) | async-done | bytes 1048608 | tf_op jit(solution)/shard_map/all_to_all | solution.py:56
  42.1 0.1 copy.25
  42.1 4.6 %all_to_all.51 = f32[2,8,1,32,1,2,2,128]{7,6,3,1,0,4,2,5:T(2,128)S(1)} all-to-all(f32[2,8,1,32,1,2,2,128]{7,6,3,1,0,4,2,5:T(2,128)S(1)} %copy.25), channel_id=1, replica_groups=mesh['groups'=2,'range'=8,'sub'=2] {'sub'}, dimensions={5} | all-to-all | bytes 2097152 | tf_op jit(solution)/shard_map/all_to_all | solution.py:55
  46.7 0.1 copy.26
  46.8 0.8 copy.27
  47.6 2.3 %gather_fusion = f32[512,2,256]{2,1,0:T(2,128)S(1)} fusion(f32[1,2,512,256]{3,1,2,0:T(2,128)S(1)} %copy.27, s32[512]{0:T(512)S(1)} %reshape.147), kind=kCustom, calls=%fused_computation | custom fusion | bytes 2101248 | tf_op jit(solution)/shard_map/vmap(jit(_take))/gather | solution.py:12
  50.0 0.1 copy.28
  50.1 0.1 broadcast_select_fusion
  50.2 1.0 %convolution_bitcast_fusion.2 = f32[256,128]{1,0:T(8,128)S(1)} fusion(f32[1,2,8,64,256]{4,3,2,1,0:T(8,128)S(1)} %broadcast_select_fusion, f32[1,8,2,64,128]{4,3,1,2,0:T(8,128)S(1)} %all_to_all.47), kind=kOutput, calls=%fused_computation.13 | convolution fusion | flops 201326592 | bytes 917504 | tf_op jit(solution)/shard_map/vmap(snk,snx->kx)/dot_general | solution.py:27
  51.2 1.0 %convolution_bitcast_fusion = f32[256,128]{1,0:T(8,128)S(1)} fusion(f32[1,2,8,64,256]{4,3,2,1,0:T(8,128)S(1)} %broadcast_select_fusion, f32[1,8,2,64,128]{4,3,1,2,0:T(8,128)S(1)} %all_to_all.47), kind=kOutput, calls=%fused_computation.11 | convolution fusion | flops 201326592 | bytes 917504 | tf_op jit(solution)/shard_map/vmap(snk,snx->kx)/dot_general | solution.py:30
  52.2 0.6 fusion.12
  52.9 0.6 fusion.2
  53.5 0.4 fusion.19
  53.9 0.4 fusion.18
  54.3 0.6 fusion.8
  54.9 1.0 %fusion.6 = f32[256,128]{1,0:T(8,128)S(1)} fusion(f32[256,128]{1,0:T(8,128)S(1)} %convolution_bitcast_fusion.2, f32[1,2,8,64,256]{4,3,2,1,0:T(8,128)S(1)} %broadcast_select_fusion, f32[1,8,2,64,128]{4,3,1,2,0:T(8,128)S(1)} %all_to_all.47), kind=kOutput, calls=%fused_computation.15 | convolution fusion | flops 201359360 | bytes 1048576 | tf_op jit(solution)/shard_map/vmap(snk,snx->kx)/dot_general | solution.py:27
  55.9 0.6 fusion.3
  56.5 0.4 fusion
  56.9 0.4 fusion.5
  57.4 1.0 %add_reduce_fusion = (f32[128]{0:T(128)S(1)}, f32[256,128]{1,0:T(8,128)S(1)}, f32[256,128]{1,0:T(8,128)S(1)}) fusion(f32[256,128]{1,0:T(8,128)S(1)} %fusion.6, f32[128]{0:T(128)S(1)} %add_rsqrt_fusion, f32[256,128]{1,0:T(8,128)S(1)} %convolution_bitcast_fusion, f32[1,8,2,64,128]{4,3,1,2,0:T(8,128)S(1)} %all_to_all.47, ...), kind=kOutput, calls=%fused_computation.36 | convolution fusion | flops 201555840 | bytes 1311744 | tf_op jit(solution)/shard_map/vmap(snk,snx->kx)/dot_general | solution.py:30
  58.4 31.6 %psum.7 = f32[128]{0:T(128)S(1)} all-reduce(f32[128]{0:T(128)S(1)} %get-tuple-element.3), channel_id=1, replica_groups=mesh['groups'=2,'range'=8,'sub'=2] {'range','sub'}, use_global_device_ids=true, to_apply=%region_2.3 | all-reduce | flops 128 | bytes 1024 | tf_op jit(solution)/shard_map/psum | solution.py:73
  90.1 0.5 broadcast_multiply_fusion.2
  90.6 0.1 copy.30
  90.7 0.1 copy.31
  90.8 0.8 pad_maximum_fusion
  91.7 0.8 pad_maximum_fusion.1
  (6 shorter events, 0.0 us)
Async XLA Ops:
  0.6 6.0 %copy-start = (f32[2,32,32,128]{3,2,1,0:T(8,128)S(1)}, f32[2,32,32,128]{3,2,1,0:T(8,128)}, u32[]{:S(2)}) copy-start(f32[2,32,32,128]{3,2,1,0:T(8,128)} %param.4) | copy-start | bytes 3145732
  3.2 5.2 %all-to-all-start.2 = ((f32[2,1,65536]{2,1,0:T(1,128)}), f32[2,1,65536]{2,1,0:T(1,128)S(1)}, u32[]{:S(2)}, u32[]{:S(2)}) async-start(f32[2,1,65536]{2,1,0:T(1,128)} %reshape.157), calls=%async_computation.2 | async-start | bytes 1048576 | tf_op jit(solution)/shard_map/all_to_all | solution.py:63
  8.2 7.6 %copy-start.2 = (s32[2]{0:T(128)S(1)}, s32[2]{0:T(128)}, u32[]{:S(2)}) copy-start(s32[2]{0:T(128)} %param.7) | copy-start | bytes 28
  8.4 7.4 %copy-start.1 = (s32[1,8,64]{2,1,0:T(8,128)S(1)}, s32[1,8,64]{2,1,0:T(8,128)}, u32[]{:S(2)}) copy-start(s32[1,8,64]{2,1,0:T(8,128)} %param.6) | copy-start | bytes 6148
  8.4 33.7 %all-to-all-start = ((f32[2,1,1,32,8,2,2,128]{7,6,3,5,0,2,1,4:T(2,128)}), f32[2,1,1,32,8,2,2,128]{7,6,3,5,0,2,1,4:T(2,128)S(1)}, u32[]{:S(2)}, u32[]{:S(2)}) async-start(f32[2,1,1,32,8,2,2,128]{7,6,3,5,0,2,1,4:T(2,128)} %copy.24), calls=%async_computation | async-start | bytes 2097152 | tf_op jit(solution)/shard_map/all_to_all | solution.py:56
where the time goes:
time: 92.9 us; the launch traced here: 92.5 us
  blocking collectives  36.2 us (39%)
  waiting for transfers between devices  19.1 us (21%)
  local copies, waits for them, and re-layouts  12.7 us (14%)
  starting transfers between devices  10.9 us (12%)
  matrix products  8.13 us (9%)
  other arithmetic  4.67 us (5%)
    psum x1, blocking collectives, body(): total = lax.psum(jnp.sum(energies, axis=0), ('range', 'sub'))  31.6 us
    all_to_all x1, waiting for transfers between devices, body(): lax.all_to_all(spread, 'range', split_axis=4, concat_axis=1, tiled=True)  18.9 us
    all_to_all x1, starting transfers between devices, body(): lax.all_to_all(spread, 'range', split_axis=4, concat_axis=1, tiled=True)  7.41 us
    all_to_all x1, blocking collectives, body(): lax.all_to_all(lax.all_to_all(spread, 'range', split_axis=4, concat_axis=...  4.58 us
    all_to_all x3, local copies, waits for them, and re-layouts, body(): lax.all_to_all(beam_weights, 'sub', split_axis=0, concat_axis=4, tiled=True)  4.18 us
    all_to_all x1, starting transfers between devices, body(): lax.all_to_all(beam_weights, 'sub', split_axis=0, concat_axis=4, tiled=True)  3.49 us
    unnamed x8, local copies, waits for them, and re-layouts  3.15 us
    gather x4, local copies, waits for them, and re-layouts, block_terms(): picked = jnp.take(snaps, chosen, axis=1)  2.5 us
  transfers between devices with their start and end apart: 2, of which 2 were waited for; matrix products, arithmetic and copies ran while one was open for 8% of the time, Pallas kernels for 0%

commit v1 on v0

--- a/solution.py
+++ b/solution.py
@@ -70,7 +70,7 @@
     beams = filts.shape[2]
     filtered = filts.reshape(blocks_dev, parts_iq, beams, GB, pulses).transpose(1, 2, 0, 3, 4)
     filtered = filtered.reshape(parts_iq, beams, gate_dev, pulses)
-    total = lax.psum(jnp.sum(energies, axis=0), ("range", "sub"))
+    total = lax.psum(lax.psum(jnp.sum(energies, axis=0), "sub"), "range")
     energy = total / (all_gates * pulses)
     return (covs, filtered, energy)
 

time: 92.9 us -> 83.2 us (0.90)
  blocking collectives: 36.2 us -> 26.5 us
    psum x1 -> x2, blocking collectives: 31.6 us -> 21.9 us  [body(): total = lax.psum(lax.psum(jnp.sum(energies, axis=0), 'sub'), 'range')]
  transfers between devices with their start and end apart: 2 -> 2, of which waited for: 2 -> 2; matrix products, arithmetic and copies ran while one was open for 8% -> 9% of each run, Pallas kernels for 0% -> 0%
where the time goes in v1:
time: 83.2 us; the launch traced here: 82.8 us
  blocking collectives  26.5 us (32%)
  waiting for transfers between devices  19.1 us (23%)
  local copies, waits for them, and re-layouts  12.7 us (15%)
  starting transfers between devices  10.9 us (13%)
  matrix products  8.13 us (10%)
  other arithmetic  4.67 us (6%)
  between operations  0.84 us (1%)
    psum x2, blocking collectives, body(): total = lax.psum(lax.psum(jnp.sum(energies, axis=0), 'sub'), 'range')  21.9 us
    all_to_all x1, waiting for transfers between devices, body(): lax.all_to_all(spread, 'range', split_axis=4, concat_axis=1, tiled=True)  18.9 us
    all_to_all x1, starting transfers between devices, body(): lax.all_to_all(spread, 'range', split_axis=4, concat_axis=1, tiled=True)  7.41 us
    all_to_all x1, blocking collectives, body(): lax.all_to_all(lax.all_to_all(spread, 'range', split_axis=4, concat_axis=...  4.58 us
    all_to_all x3, local copies, waits for them, and re-layouts, body(): lax.all_to_all(beam_weights, 'sub', split_axis=0, concat_axis=4, tiled=True)  4.18 us
    all_to_all x1, starting transfers between devices, body(): lax.all_to_all(beam_weights, 'sub', split_axis=0, concat_axis=4, tiled=True)  3.49 us
    unnamed x8, local copies, waits for them, and re-layouts  3.15 us
    gather x4, local copies, waits for them, and re-layouts, block_terms(): picked = jnp.take(snaps, chosen, axis=1)  2.5 us
  transfers between devices with their start and end apart: 2, of which 2 were waited for; matrix products, arithmetic and copies ran while one was open for 9% of the time, Pallas kernels for 0%

profile of v1, /device:TPU:0, one launch (start us, length us, event | category | flops | bytes accessed | tf_op | source)
XLA Modules:
  0.0 82.8 jit_solution(17140016756013137974)
XLA Ops:
  0.6 0.0 copy-start
  0.6 2.5 %reshape.157 = f32[2,1,65536]{2,1,0:T(1,128)} reshape(f32[2,8,2,64,64]{4,3,2,1,0:T(8,128)} %param.5) | data formatting | bytes 1048576
  3.2 3.5 %all-to-all-start.2 = ((f32[2,1,65536]{2,1,0:T(1,128)}), f32[2,1,65536]{2,1,0:T(1,128)S(1)}, u32[]{:S(2)}, u32[]{:S(2)}) async-start(f32[2,1,65536]{2,1,0:T(1,128)} %reshape.157), calls=%async_computation.2 | async-start | bytes 1048576 | tf_op jit(solution)/shard_map/all_to_all | solution.py:63
  6.6 0.0 copy-done
  6.7 1.6 %copy.24 = f32[2,1,1,32,8,2,2,128]{7,6,3,5,0,2,1,4:T(2,128)} copy(f32[2,1,1,32,8,2,2,128]{7,6,5,4,3,0,2,1:T(2,128)S(1)} %bitcast.103) | data formatting | bytes 2097152 | tf_op jit(solution)/shard_map/reshape | solution.py:54
  8.2 0.0 copy-start.2
  8.2 0.2 all-to-all-done.2
  8.4 0.0 copy-start.1
  8.4 7.4 %all-to-all-start = ((f32[2,1,1,32,8,2,2,128]{7,6,3,5,0,2,1,4:T(2,128)}), f32[2,1,1,32,8,2,2,128]{7,6,3,5,0,2,1,4:T(2,128)S(1)}, u32[]{:S(2)}, u32[]{:S(2)}) async-start(f32[2,1,1,32,8,2,2,128]{7,6,3,5,0,2,1,4:T(2,128)} %copy.24), calls=%async_computation | async-start | bytes 2097152 | tf_op jit(solution)/shard_map/all_to_all | solution.py:56
  15.8 0.0 copy-done.2
  15.8 0.0 copy-done.1
  15.9 0.1 reshape.147
  15.9 0.5 broadcast.75
  16.4 2.3 %reduce.5 = f32[2,65536]{1,0:T(2,128)S(1)} reduce(f32[2,1,65536]{2,1,0:T(1,128)S(1)} %all-to-all-done.2, f32[]{:T(128)} %broadcast.75), dimensions={1}, to_apply=%all_to_all.44.reduce_sub_computation | reduce | bytes 1048580 | tf_op jit(solution)/shard_map/all_to_all | solution.py:63
  18.8 0.6 reshape.158
  19.4 1.9 %copy.29 = f32[1,8,2,64,2,64]{5,4,3,1,2,0:T(2,128)} copy(f32[1,8,2,64,2,64]{5,3,2,1,4,0:T(8,128)S(1)} %bitcast.98) | data formatting | bytes 1048576 | tf_op jit(solution)/shard_map/all_to_all | solution.py:63
  21.2 1.8 %all_to_all.47 = f32[1,8,2,64,128]{4,3,1,2,0:T(8,128)S(1)} reshape(f32[1,8,2,64,2,64]{5,4,3,1,2,0:T(2,128)} %copy.29) | data formatting | bytes 1048576 | tf_op jit(solution)/shard_map/all_to_all | solution.py:63
  23.1 0.1 broadcast_bitcast_fusion
  23.1 18.9 %all-to-all-done = f32[2,1,1,32,8,2,2,128]{7,6,3,5,0,2,1,4:T(2,128)S(1)} async-done(((f32[2,1,1,32,8,2,2,128]{7,6,3,5,0,2,1,4:T(2,128)}), f32[2,1,1,32,8,2,2,128]{7,6,3,5,0,2,1,4:T(2,128)S(1)}, u32[]{:S(2)}, u32[]{:S(2)}) %all-to-all-start) | async-done | bytes 1048608 | tf_op jit(solution)/shard_map/all_to_all | solution.py:56
  42.1 0.1 copy.25
  42.1 4.6 %all_to_all.51 = f32[2,8,1,32,1,2,2,128]{7,6,3,1,0,4,2,5:T(2,128)S(1)} all-to-all(f32[2,8,1,32,1,2,2,128]{7,6,3,1,0,4,2,5:T(2,128)S(1)} %copy.25), channel_id=1, replica_groups=mesh['groups'=2,'range'=8,'sub'=2] {'sub'}, dimensions={5} | all-to-all | bytes 2097152 | tf_op jit(solution)/shard_map/all_to_all | solution.py:55
  46.7 0.1 copy.26
  46.8 0.8 copy.27
  47.6 2.3 %gather_fusion = f32[512,2,256]{2,1,0:T(2,128)S(1)} fusion(f32[1,2,512,256]{3,1,2,0:T(2,128)S(1)} %copy.27, s32[512]{0:T(512)S(1)} %reshape.147), kind=kCustom, calls=%fused_computation | custom fusion | bytes 2101248 | tf_op jit(solution)/shard_map/vmap(jit(_take))/gather | solution.py:12
  50.0 0.1 copy.28
  50.1 0.1 broadcast_select_fusion
  50.2 1.0 %convolution_bitcast_fusion.2 = f32[256,128]{1,0:T(8,128)S(1)} fusion(f32[1,2,8,64,256]{4,3,2,1,0:T(8,128)S(1)} %broadcast_select_fusion, f32[1,8,2,64,128]{4,3,1,2,0:T(8,128)S(1)} %all_to_all.47), kind=kOutput, calls=%fused_computation.13 | convolution fusion | flops 201326592 | bytes 917504 | tf_op jit(solution)/shard_map/vmap(snk,snx->kx)/dot_general | solution.py:27
  51.2 1.0 %convolution_bitcast_fusion = f32[256,128]{1,0:T(8,128)S(1)} fusion(f32[1,2,8,64,256]{4,3,2,1,0:T(8,128)S(1)} %broadcast_select_fusion, f32[1,8,2,64,128]{4,3,1,2,0:T(8,128)S(1)} %all_to_all.47), kind=kOutput, calls=%fused_computation.11 | convolution fusion | flops 201326592 | bytes 917504 | tf_op jit(solution)/shard_map/vmap(snk,snx->kx)/dot_general | solution.py:30
  52.2 0.6 fusion.12
  52.9 0.6 fusion.2
  53.5 0.4 fusion.19
  53.9 0.4 fusion.18
  54.3 0.6 fusion.8
  54.9 1.0 %fusion.6 = f32[256,128]{1,0:T(8,128)S(1)} fusion(f32[256,128]{1,0:T(8,128)S(1)} %convolution_bitcast_fusion.2, f32[1,2,8,64,256]{4,3,2,1,0:T(8,128)S(1)} %broadcast_select_fusion, f32[1,8,2,64,128]{4,3,1,2,0:T(8,128)S(1)} %all_to_all.47), kind=kOutput, calls=%fused_computation.15 | convolution fusion | flops 201359360 | bytes 1048576 | tf_op jit(solution)/shard_map/vmap(snk,snx->kx)/dot_general | solution.py:27
  55.9 0.6 fusion.3
  56.5 0.4 fusion
  56.9 0.4 fusion.5
  57.4 1.0 %add_reduce_fusion = (f32[128]{0:T(128)S(1)}, f32[256,128]{1,0:T(8,128)S(1)}, f32[256,128]{1,0:T(8,128)S(1)}) fusion(f32[256,128]{1,0:T(8,128)S(1)} %fusion.6, f32[128]{0:T(128)S(1)} %add_rsqrt_fusion, f32[256,128]{1,0:T(8,128)S(1)} %convolution_bitcast_fusion, f32[1,8,2,64,128]{4,3,1,2,0:T(8,128)S(1)} %all_to_all.47, ...), kind=kOutput, calls=%fused_computation.36 | convolution fusion | flops 201555840 | bytes 1311744 | tf_op jit(solution)/shard_map/vmap(snk,snx->kx)/dot_general | solution.py:30
  58.4 2.5 %psum.14 = f32[128]{0:T(128)S(1)} all-reduce(f32[128]{0:T(128)S(1)} %get-tuple-element.3), channel_id=1, replica_groups=mesh['groups'=2,'range'=8,'sub'=2] {'sub'}, use_global_device_ids=true, to_apply=%region_2.3 | all-reduce | flops 128 | bytes 1024 | tf_op jit(solution)/shard_map/psum | solution.py:73
  60.9 19.5 %psum.15 = f32[128]{0:T(128)S(1)} all-reduce(f32[128]{0:T(128)S(1)} %psum.14), channel_id=1, replica_groups=mesh['groups'=2,'range'=8,'sub'=2] {'range'}, use_global_device_ids=true, to_apply=%region_3.4 | all-reduce | flops 128 | bytes 1024 | tf_op jit(solution)/shard_map/psum | solution.py:73
  80.3 0.5 broadcast_multiply_fusion.2
  80.9 0.1 copy.30
  81.0 0.1 copy.31
  81.1 0.8 %pad_maximum_fusion = f32[1,8,64,128]{3,2,1,0:T(8,128)} fusion(f32[1,8,64,64]{3,2,1,0:T(8,128)S(1)} %bitcast.102, f32[1,8,64,64]{3,2,1,0:T(8,128)S(1)} %bitcast.96), kind=kLoop, calls=%fused_computation.28 | loop fusion | flops 65536 | bytes 524288 | tf_op jit(solution)/shard_map/vmap()/concatenate | solution.py:43
  81.9 0.8 pad_maximum_fusion.1
  (6 shorter events, 0.0 us)
Async XLA Ops:
  0.6 6.0 %copy-start = (f32[2,32,32,128]{3,2,1,0:T(8,128)S(1)}, f32[2,32,32,128]{3,2,1,0:T(8,128)}, u32[]{:S(2)}) copy-start(f32[2,32,32,128]{3,2,1,0:T(8,128)} %param.4) | copy-start | bytes 3145732
  3.2 5.2 %all-to-all-start.2 = ((f32[2,1,65536]{2,1,0:T(1,128)}), f32[2,1,65536]{2,1,0:T(1,128)S(1)}, u32[]{:S(2)}, u32[]{:S(2)}) async-start(f32[2,1,65536]{2,1,0:T(1,128)} %reshape.157), calls=%async_computation.2 | async-start | bytes 1048576 | tf_op jit(solution)/shard_map/all_to_all | solution.py:63
  8.2 7.6 %copy-start.2 = (s32[2]{0:T(128)S(1)}, s32[2]{0:T(128)}, u32[]{:S(2)}) copy-start(s32[2]{0:T(128)} %param.7) | copy-start | bytes 28
  8.4 7.4 %copy-start.1 = (s32[1,8,64]{2,1,0:T(8,128)S(1)}, s32[1,8,64]{2,1,0:T(8,128)}, u32[]{:S(2)}) copy-start(s32[1,8,64]{2,1,0:T(8,128)} %param.6) | copy-start | bytes 6148
  8.4 33.7 %all-to-all-start = ((f32[2,1,1,32,8,2,2,128]{7,6,3,5,0,2,1,4:T(2,128)}), f32[2,1,1,32,8,2,2,128]{7,6,3,5,0,2,1,4:T(2,128)S(1)}, u32[]{:S(2)}, u32[]{:S(2)}) async-start(f32[2,1,1,32,8,2,2,128]{7,6,3,5,0,2,1,4:T(2,128)} %copy.24), calls=%async_computation | async-start | bytes 2097152 | tf_op jit(solution)/shard_map/all_to_all | solution.py:56
